TPU v7x, 32 devices: a whole 2x2x4 slice. The times are simulated.
32 devices in a mesh: gx: 4 (over z), gy: 2 (over x), gz: 4 (over y, core).
Axes of the slice: x: 2, y: 2, z: 4, core: 2. Of those that a mesh axis runs over, the one named last changes fastest.
Arguments:
- attn_out: bfloat16 [16384, 8192], P('gx', ('gy', 'gz')), may hold values from -6 to 6
- out_grad: bfloat16 [16384, 8192], P('gx', ('gz', 'gy')), may hold values from -0.046875 to 0.046875
- valid_counts: int32 [16], P('gx'), may hold values from 128 to 1024
Outputs:
- weight_grad: float32 [8192, 8192], P(('gy', 'gx'), 'gz')
Inputs may be any that keep to these rules, and one draw needn't show every extreme that they name: `valid_counts`: valid tokens of a packed row come first, padding after.
All inputs are finite; a program needn't handle non-finite values.
Results may differ from a plain program's by a relative error of at most 0.0003.
Values may be sent and summed in bfloat16 or wider, within the bound.
No kernel may reach another device: no remote copies, remote signals or barrier semaphores. Data moves between devices by JAX's collectives and lax.ppermute only.
A program may use at most 192 MiB of HBM per device.

v0:
```python
import jax
import jax.numpy as jnp
from jax import lax
from jax.sharding import PartitionSpec as P


def transpose_product(inputs, grads):
    return lax.dot_general(
        inputs, grads, (((0,), (0,)), ((), ())), preferred_element_type=jnp.float32
    )


def shards(attn_out, out_grad, valid_counts):
    rows_here = valid_counts.shape[0]
    slot_count = attn_out.shape[0] // rows_here
    positions = lax.broadcasted_iota(jnp.int32, (rows_here, slot_count), 1)
    kept_rows = (positions < valid_counts[:, None]).reshape(-1)
    gathered_inputs = lax.all_gather(attn_out, "gz", axis=1, tiled=True)
    gathered_grads = lax.all_gather(out_grad, "gy", axis=1, tiled=True)
    masked = jnp.where(kept_rows[:, None], gathered_grads, jnp.zeros((), gathered_grads.dtype))
    partial_grad = transpose_product(gathered_inputs, masked)
    return lax.psum_scatter(partial_grad, "gx", scatter_dimension=0, tiled=True)


def solution(mesh):
    in_specs = (P("gx", ("gy", "gz")), P("gx", ("gz", "gy")), P("gx"))
    out_specs = P(("gy", "gx"), "gz")
    return jax.shard_map(shards, mesh=mesh, in_specs=in_specs, out_specs=out_specs, check_vma=False)
```

profile of v0, /device:TPU:0, one launch (start us, length us, event | category | flops | bytes accessed | tf_op | source)
XLA Modules:
  0.0 1061.9 jit_solution(18123328808910169511)
XLA Ops:
  6.5 0.0 copy-start
  6.5 0.0 all-gather.3.cloned.1.call-start
  6.5 0.7 all-gather.3.cloned.1.call-update
  7.3 0.0 all-gather.5.cloned.1.call-start
  7.3 0.7 all-gather.5.cloned.1.call-update
  8.0 0.0 reduce-scatter.2.cloned.1.call-start
  8.1 0.0 copy-done
  8.1 0.1 fusion.3
  8.2 202.3 %all-gather.3.cloned.1.call-done = bf16[4096,2048]{1,0:T(8,128)(2,1)} async-done(((bf16[4096,1024]{1,0:T(8,128)(2,1)}), bf16[4096,2048]{1,0:T(8,128)(2,1)}) %all-gather.3.cloned.1.call-update) | async-done | bytes 16777232 | tf_op jit(solution)/shard_map/all_gather | solution.py:19
  210.5 203.1 %all-gather.5.cloned.1.call-done = bf16[4096,4096]{1,0:T(8,128)(2,1)} async-done(((bf16[4096,1024]{1,0:T(8,128)(2,1)}), bf16[4096,4096]{1,0:T(8,128)(2,1)}) %all-gather.5.cloned.1.call-update) | async-done | bytes 33554448 | tf_op jit(solution)/shard_map/all_gather | solution.py:18
  413.6 80.3 %convolution_bitcast_fusion = f32[4096,2048]{0,1:T(8,128)} fusion(bf16[4096,4096]{1,0:T(8,128)(2,1)} %all-gather.5.cloned.1.call-done, bf16[4096,2048]{1,0:T(8,128)(2,1)} %all-gather.3.cloned.1.call-done, pred[4096]{0:T(1024)(128)(4,1)S(1)} %bitcast.10), kind=kOutput, calls=%fused_computation | convolution fusion | flops 68727865344 | bytes 83890176 | tf_op jit(solution)/shard_map/dot_general | solution.py:8
  493.9 0.0 reduce-scatter.2.cloned.1.call-update
  493.9 552.4 %reduce-scatter.2.cloned.1.call-done = f32[1024,2048]{0,1:T(8,128)} async-done(((f32[4096,2048]{0,1:T(8,128)}), f32[1024,2048]{0,1:T(8,128)}) %reduce-scatter.2.cloned.1.call-update) | async-done | bytes 8388624 | tf_op jit(solution)/shard_map/reduce_scatter | solution.py:22
  1046.3 9.1 copy.4
  (1 shorter events, 0.0 us)
Async XLA Ops:
  6.5 1.5 copy-start
  6.5 203.9 %all-gather.3.cloned.1.call-start = ((), (), s32[]{:S(2)}) async-start(), calls=%async_computation.1 | async-start | bytes 25165824 | tf_op jit(solution)/shard_map/all_gather | solution.py:19
  7.3 406.3 %all-gather.5.cloned.1.call-start = ((), (), s32[]{:S(2)}) async-start(), calls=%async_computation.2 | async-start | bytes 41943040 | tf_op jit(solution)/shard_map/all_gather | solution.py:18
  8.0 1038.2 %reduce-scatter.2.cloned.1.call-start = ((), (), s32[]{:S(2)}) async-start(), calls=%async_computation.3 | async-start | bytes 41943040 | tf_op jit(solution)/shard_map/reduce_scatter | solution.py:22
Sparse Core Ops, SparseCore 0:
  8.9 201.5 all-gather.2
  212.1 201.4 all-gather.4
  494.0 552.2 reduce-scatter.1
where the time goes:
time: 1060 us
  waiting for transfers between devices  959 us (90%)
  matrix products  80.3 us (8%)
  between operations  13.1 us (1%)
    reduce_scatter x1, waiting for transfers between devices, shards(): return lax.psum_scatter(partial_grad, 'gx', scatter_dimension=0, tiled=True)  552 us
    all_gather x1, waiting for transfers between devices, shards(): gathered_inputs = lax.all_gather(attn_out, 'gz', axis=1, tiled=True)  203 us
    all_gather x1, waiting for transfers between devices, shards(): gathered_grads = lax.all_gather(out_grad, 'gy', axis=1, tiled=True)  202 us
    dot_general x1, matrix products, transpose_product(): lax.dot_general(inputs, grads, (((0,), (0,)), ((), ())), preferred_elemen...  80.3 us
  transfers between devices with their start and end apart: 3, of which 3 were waited for; matrix products, arithmetic and copies ran while one was open for 0% of the time, Pallas kernels for 0%

commit v1 on v0

--- a/solution.py
+++ b/solution.py
@@ -2,6 +2,16 @@
 import jax.numpy as jnp
 from jax import lax
 from jax.sharding import PartitionSpec as P
+
+
+def gather_by_hops(array, axis, along):
+    size = lax.axis_size(axis)
+    current, blocks = (array, [array])
+    for _ in range(size - 1):
+        current = lax.ppermute(current, axis, [(i, (i + 1) % size) for i in range(size)])
+        blocks.insert(0, current)
+    merged = jnp.concatenate(blocks, axis=along)
+    return jnp.roll(merged, (lax.axis_index(axis) + 1) * array.shape[along], axis=along)
 
 
 def transpose_product(inputs, grads):
@@ -15,7 +25,7 @@
     slot_count = attn_out.shape[0] // rows_here
     positions = lax.broadcasted_iota(jnp.int32, (rows_here, slot_count), 1)
     kept_rows = (positions < valid_counts[:, None]).reshape(-1)
-    gathered_inputs = lax.all_gather(attn_out, "gz", axis=1, tiled=True)
+    gathered_inputs = gather_by_hops(attn_out, "gz", 1)
     gathered_grads = lax.all_gather(out_grad, "gy", axis=1, tiled=True)
     masked = jnp.where(kept_rows[:, None], gathered_grads, jnp.zeros((), gathered_grads.dtype))
     partial_grad = transpose_product(gathered_inputs, masked)

time: 1060 us -> 989 us (0.933)
  waiting for transfers between devices: 959 us -> 833 us
  local copies, waits for them, and re-layouts: 9.14 us -> 60.5 us
    ppermute x0 -> x3, waiting for transfers between devices: none -> 279 us  [gather_by_hops(): lax.ppermute(current, axis, [(i, (i + 1) % size) for i in range(size)])]
    all_gather x1 -> x0, waiting for transfers between devices: 203 us -> none  [shards(): gathered_inputs = lax.all_gather(attn_out, 'gz', axis=1, tiled=True)]
    all_gather x1, waiting for transfers between devices: 202 us -> 0.01 us  [shards(): gathered_grads = lax.all_gather(out_grad, 'gy', axis=1, tiled=True)]
    unnamed x3 -> x8, local copies, waits for them, and re-layouts: 0.01 us -> 53 us
  transfers between devices with their start and end apart: 3 -> 5, of which waited for: 3 -> 4; matrix products, arithmetic and copies ran while one was open for 0% -> 6% of each run, Pallas kernels for 0% -> 0%
where the time goes in v1:
time: 989 us
  waiting for transfers between devices  833 us (84%)
  matrix products  80.1 us (8%)
  local copies, waits for them, and re-layouts  60.5 us (6%)
  between operations  13.4 us (1%)
    reduce_scatter x1, waiting for transfers between devices, shards(): return lax.psum_scatter(partial_grad, 'gx', scatter_dimension=0, tiled=True)  554 us
    ppermute x3, waiting for transfers between devices, gather_by_hops(): lax.ppermute(current, axis, [(i, (i + 1) % size) for i in range(size)])  279 us
    dot_general x1, matrix products, transpose_product(): lax.dot_general(inputs, grads, (((0,), (0,)), ((), ())), preferred_elemen...  80.1 us
    unnamed x8, local copies, waits for them, and re-layouts  53 us
  transfers between devices with their start and end apart: 5, of which 4 were waited for; matrix products, arithmetic and copies ran while one was open for 6% of the time, Pallas kernels for 0%

profile of v1, /device:TPU:0, one launch (start us, length us, event | category | flops | bytes accessed | tf_op | source)
XLA Modules:
  0.0 988.7 jit_solution(15914844357504711580)
XLA Ops:
  6.5 0.0 all-gather.2.cloned.1.call-start
  6.5 0.5 collective-permute-start
  7.0 93.4 %collective-permute-done = bf16[4096,1024]{1,0:T(8,128)(2,1)} collective-permute-done((bf16[4096,1024]{1,0:T(8,128)(2,1)}, bf16[4096,1024]{1,0:T(8,128)(2,1)}, u32[]{:S(2)}, u32[]{:S(2)}) %collective-permute-start) | collective-permute-done | bytes 8388640 | tf_op jit(solution)/shard_map/ppermute | solution.py:11
  100.4 0.0 collective-permute-start.1
  100.4 0.0 all-gather.2.cloned.1.call-update
  100.4 0.0 reduce-scatter.2.cloned.1.call-start
  100.5 93.1 %collective-permute-done.1 = bf16[4096,1024]{1,0:T(8,128)(2,1)} collective-permute-done((bf16[4096,1024]{1,0:T(8,128)(2,1)}, bf16[4096,1024]{1,0:T(8,128)(2,1)}, u32[]{:S(2)}, u32[]{:S(2)}) %collective-permute-start.1) | collective-permute-done | bytes 8388640 | tf_op jit(solution)/shard_map/ppermute | solution.py:11
  193.6 0.0 collective-permute-start.2
  193.6 0.7 fusion.5
  194.4 92.4 %collective-permute-done.2 = bf16[4096,1024]{1,0:T(8,128)(2,1)} collective-permute-done((bf16[4096,1024]{1,0:T(8,128)(2,1)}, bf16[4096,1024]{1,0:T(8,128)(2,1)}, u32[]{:S(2)}, u32[]{:S(2)}) %collective-permute-start.2) | collective-permute-done | bytes 8388640 | tf_op jit(solution)/shard_map/ppermute | solution.py:11
  286.8 7.5 constant_dynamic-update-slice_fusion.7
  294.3 7.6 constant_dynamic-update-slice_fusion.6
  301.9 7.6 constant_dynamic-update-slice_fusion.5
  309.6 7.6 constant_dynamic-update-slice_fusion.4
  317.1 7.5 constant_dynamic-update-slice_fusion.3
  324.7 7.6 constant_dynamic-update-slice_fusion.2
  332.2 7.5 constant_dynamic-update-slice_fusion.1
  339.7 7.6 constant_dynamic-update-slice_fusion
  347.3 0.0 all-gather.2.cloned.1.call-done
  347.3 80.1 %fusion = f32[4096,2048]{1,0:T(8,128)} fusion(bf16[4096,8192]{1,0:T(8,128)(2,1)} %constant_dynamic-update-slice_fusion, s32[]{:T(128)S(6)} %select_n.18, bf16[4096,2048]{1,0:T(8,128)(2,1)} %all-gather.2.cloned.1.call-done, pred[4096]{0:T(1024)(128)(4,1)S(1)} %bitcast.5), kind=kOutput, calls=%fused_computation | convolution fusion | flops 68727865344 | bytes 83890176 | tf_op jit(solution)/shard_map/dot_general | solution.py:18
  427.4 0.0 reduce-scatter.2.cloned.1.call-update
  427.5 554.4 %reduce-scatter.2.cloned.1.call-done = f32[1024,2048]{1,0:T(8,128)} async-done(((f32[4096,2048]{1,0:T(8,128)}), f32[1024,2048]{1,0:T(8,128)}) %reduce-scatter.2.cloned.1.call-update) | async-done | bytes 8388624 | tf_op jit(solution)/shard_map/reduce_scatter | solution.py:32
  (1 shorter events, 0.0 us)
Async XLA Ops:
  6.5 340.8 %all-gather.2.cloned.1.call-start = ((), (), s32[]{:S(2)}) async-start(), calls=%async_computation.1 | async-start | bytes 25165824 | tf_op jit(solution)/shard_map/all_gather | solution.py:29
  6.5 93.9 %collective-permute-start = (bf16[4096,1024]{1,0:T(8,128)(2,1)}, bf16[4096,1024]{1,0:T(8,128)(2,1)}, u32[]{:S(2)}, u32[]{:S(2)}) collective-permute-start(bf16[4096,1024]{1,0:T(8,128)(2,1)} %param.3), channel_id=1, source_target_pairs={{0,1},{1,2},{2,3},{3,0},{4,5},{5,6},{6,7},{7,4},{8,9},{9,10},{10,1... | collective-permute-start | bytes 25165832 | tf_op jit(solution)/shard_map/ppermute | solution.py:11
  100.4 93.2 %collective-permute-start.1 = (bf16[4096,1024]{1,0:T(8,128)(2,1)}, bf16[4096,1024]{1,0:T(8,128)(2,1)}, u32[]{:S(2)}, u32[]{:S(2)}) collective-permute-start(bf16[4096,1024]{1,0:T(8,128)(2,1)} %collective-permute-done), channel_id=1, source_target_pairs={{0,1},{1,2},{2,3},{3,0},{4,5},{5,6},{6,7},{7,4},{8,9},{9,10},{10,1... | collective-permute-start | bytes 25165832 | tf_op jit(solution)/shard_map/ppermute | solution.py:11
  100.4 881.4 %reduce-scatter.2.cloned.1.call-start = ((), (), s32[]{:S(2)}) async-start(), calls=%async_computation.2 | async-start | bytes 41943040 | tf_op jit(solution)/shard_map/reduce_scatter | solution.py:32
  193.6 93.2 %collective-permute-start.2 = (bf16[4096,1024]{1,0:T(8,128)(2,1)}, bf16[4096,1024]{1,0:T(8,128)(2,1)}, u32[]{:S(2)}, u32[]{:S(2)}) collective-permute-start(bf16[4096,1024]{1,0:T(8,128)(2,1)} %collective-permute-done.1), channel_id=1, source_target_pairs={{0,1},{1,2},{2,3},{3,0},{4,5},{5,6},{6,7},{7,4},{8,9},{9,10},{10,1... | collective-permute-start | bytes 25165832 | tf_op jit(solution)/shard_map/ppermute | solution.py:11
Sparse Core Ops, SparseCore 0:
  100.6 201.1 all-gather.1
  427.6 554.2 reduce-scatter.1
